TPU v7x, 256 devices: a 4x2x16 block of a 4x16x16 slice. The times are simulated.
256 devices in a mesh: groups: 2 (over y), ep: 16 (over z), node: 8 (over x, core).
Axes of the slice: x: 4, y: 2, z: 16, core: 2. Of those that a mesh axis runs over, the one named last changes fastest.
The devices are a block of a 4x16x16 slice.
Arguments:
- queries: bfloat16 [4096, 64, 576], P(('groups', 'ep'), 'node'), parts along dimension 0, may hold values from -16 to 16
- latent_kv: bfloat16 [4096, 576], P(('groups', 'ep')), parts along dimension 0, may hold values from -4 to 4
- w_value: bfloat16 [64, 512, 128], P('node'), may hold values from -0.25 to 0.25
- moe_tokens: bfloat16 [1024, 4096], P(('groups', 'ep')), parts along dimension 0, may hold values from -6 to 6
- routes: int32 [1024, 8], P(('groups', 'ep')), parts along dimension 0, may hold values from 0 to 15, all different within a row; in each aligned block of 32 rows (0 to 31, 32 to 63, ...) at most 24 rows name the same one
- router: bfloat16 [4096, 16], replicated, may hold values from -0.25 to 0.25
- w_gate: bfloat16 [16, 4096, 2048], P('ep', None, 'node'), may hold values from -0.09375 to 0.09375
- w_up: bfloat16 [16, 4096, 2048], P('ep', None, 'node'), may hold values from -0.09375 to 0.09375
- w_down: bfloat16 [16, 2048, 4096], P('ep', 'node'), may hold values from -0.1875 to 0.1875
Outputs:
- attention_out: bfloat16 [4096, 8192], P(('groups', 'ep'), 'node'), parts along dimension 0
- moe_out: bfloat16 [1024, 4096], P(('groups', 'ep'), 'node'), parts along dimension 0
There are 2 independent parts, one for each index of `groups`. A program takes and returns all parts, laid end to end along the dimension named above; an argument that names none is the same for every part. Nothing has to cross between parts.
Inputs may be any that keep to these rules, and one draw needn't show every extreme that they name: `routes`: each row names 8 different experts; among the 32 rows of one index of ep no expert is named by more than 24 rows, a bound that some block reaches of them.
All inputs are finite; a program needn't handle non-finite values.
Results may differ from a plain program's by a relative error of at most 0.015.
Values may be sent and summed in bfloat16 or wider, within the bound.
A program may use at most 64 MiB of HBM per device.

v0:
```python
import jax
import jax.numpy as jnp
from jax import lax
from jax.sharding import Mesh
from jax.sharding import PartitionSpec as P

NODE = ("node_0", "node_1")


ROUTED_SCALE = 2.5
NEGATIVE = -1e30


def in_order(tiles, dim):
    tiles = jnp.moveaxis(tiles, 0, dim)
    dims = tiles.shape
    return tiles.reshape(*dims[:dim], dims[dim] * dims[dim + 1], *dims[dim + 2 :])


def all_blocks(shard, axes, sequence):
    tiles = shard
    for k in sequence:
        tiles = lax.all_gather(tiles, axes[k])
    done = sequence[::-1]
    back = [done.index(k) for k in range(len(axes))]
    tiles = tiles.transpose(*back, *range(len(axes), tiles.ndim))
    return tiles.reshape(-1, *shard.shape)


def whole_of(shard, axes, sequence, dim):
    return in_order(all_blocks(shard, axes, sequence), dim)


def split_up(shard, dim, length):
    before, after = (shard.shape[:dim], shard.shape[dim + 1 :])
    return jnp.moveaxis(shard.reshape(*before, length, -1, *after), dim, 0)


def sent_and_summed(shard, axis, dim):
    tiles = split_up(shard, dim, lax.axis_size(axis))
    arrived = lax.all_to_all(tiles, axis, split_axis=0, concat_axis=0, tiled=True)
    return arrived.astype(jnp.float32).sum(axis=0)


def attend_block(carry, piece, queries, first_query, scale, latent_width):
    running_max, running_total, context = carry
    query_pos = first_query + lax.iota(jnp.int32, queries.shape[0])
    key_pos = lax.iota(jnp.int32, piece.shape[0])
    visible = key_pos[None, None, :] <= query_pos[:, None, None]
    scores = jnp.einsum("qhc,kc->qhk", queries, piece, preferred_element_type=jnp.float32) * scale
    scores = jnp.where(visible, scores, NEGATIVE)
    new_max = jnp.maximum(running_max, jnp.max(scores, axis=2))
    raised = jnp.where(visible, jnp.exp(scores - new_max[:, :, None]), 0.0)
    new_total = jnp.sum(raised, axis=2)
    values = piece[:, :latent_width]
    added = jnp.einsum(
        "qhk,kc->qhc", raised.astype(jnp.bfloat16), values, preferred_element_type=jnp.float32
    )
    return (new_max, new_total, added)


def per_device(queries, latent_kv, w_value, moe_tokens, routes, router, w_gate, w_up, w_down):
    seq_dev, heads_dev, width = queries.shape
    latent_width = w_value.shape[1]
    value_width = w_value.shape[2]
    scale = (value_width + width - latent_width) ** (-0.5)
    first_query = lax.axis_index("ep") * seq_dev
    last_query = first_query + seq_dev - 1
    start_carry = (
        jnp.full((seq_dev, heads_dev), NEGATIVE, jnp.float32),
        jnp.zeros((seq_dev, heads_dev), jnp.float32),
        jnp.zeros((seq_dev, heads_dev, latent_width), jnp.float32),
    )
    piece = lax.all_gather(latent_kv, "ep", axis=0, tiled=True)
    running = lax.cond(
        jnp.int32(0) <= last_query,
        lambda inner: attend_block(inner, piece, queries, first_query, scale, latent_width),
        lambda inner: inner,
        start_carry,
    )
    context = (running[2] / running[1][:, :, None]).astype(jnp.bfloat16)
    attention_out = jnp.einsum("qhc,hcv->qhv", context, w_value, preferred_element_type=jnp.float32)
    attention_out = attention_out.astype(jnp.bfloat16).reshape(seq_dev, heads_dev * value_width)
    tokens_dev, top = routes.shape
    model_width = moe_tokens.shape[1]
    local_experts = w_gate.shape[0]
    ep_size = lax.axis_size("ep")
    experts = local_experts * ep_size
    capacity = min(tokens_dev, 3 * tokens_dev * top // (2 * experts))
    logits = jnp.dot(moe_tokens, router, preferred_element_type=jnp.float32)
    affinity = jax.nn.sigmoid(logits)
    chosen = jnp.take_along_axis(affinity, routes, axis=1)
    gates = ROUTED_SCALE * chosen / jnp.sum(chosen, axis=1, keepdims=True)
    expert_range = lax.iota(jnp.int32, experts)
    member = jnp.any(routes[:, :, None] == expert_range[None, None, :], axis=1).astype(jnp.int32)
    before = jnp.cumsum(member, axis=0) - member
    slots = jnp.take_along_axis(before, routes, axis=1)
    flat_slot = routes * capacity + slots
    token_ids = jnp.broadcast_to(lax.iota(jnp.int32, tokens_dev)[:, None], routes.shape)
    slot_token = (
        jnp.zeros((experts * capacity,), jnp.int32)
        .at[flat_slot.reshape(-1)]
        .set(token_ids.reshape(-1))
    )
    slot_used = jnp.zeros((experts * capacity,), jnp.int32).at[flat_slot.reshape(-1)].set(1)
    share_width = model_width // lax.axis_size(NODE)
    source = lax.dynamic_slice_in_dim(
        moe_tokens, lax.axis_index(NODE) * share_width, share_width, 1
    )
    outgoing = jnp.where(slot_used[:, None] > 0, source[slot_token], jnp.zeros((), jnp.bfloat16))
    outgoing = outgoing.reshape(ep_size, local_experts, capacity, source.shape[1])
    arrived = lax.all_to_all(outgoing, "ep", split_axis=0, concat_axis=0, tiled=True)
    arrived = whole_of(arrived, NODE, (0, 1), 3)
    gate = jnp.einsum("sjcd,jdf->sjcf", arrived, w_gate, preferred_element_type=jnp.float32)
    upward = jnp.einsum("sjcd,jdf->sjcf", arrived, w_up, preferred_element_type=jnp.float32)
    hidden = (jax.nn.silu(gate) * upward).astype(jnp.bfloat16)
    partial_value = jnp.einsum(
        "sjcf,jfd->sjcd", hidden, w_down, preferred_element_type=jnp.float32
    ).astype(jnp.bfloat16)
    summed = sent_and_summed(partial_value.astype(jnp.float32).astype(jnp.bfloat16), NODE, 3)
    returned = lax.all_to_all(
        summed.astype(jnp.bfloat16), "ep", split_axis=0, concat_axis=0, tiled=True
    ).astype(summed.dtype)
    returned = returned.reshape(experts * capacity, returned.shape[3])
    picked = returned[flat_slot]
    weighted = gates[:, 0:1] * picked[:, 0]
    for column in range(1, top):
        weighted = weighted + gates[:, column : column + 1] * picked[:, column]
    moe_out = weighted.astype(jnp.bfloat16)
    return (attention_out, moe_out)


def solution(mesh):
    torus = Mesh(
        mesh.devices.reshape(mesh.shape["groups"], mesh.shape["ep"], 4, 2),
        ("groups", "ep", "node_0", "node_1"),
    )
    placed = (
        P(("groups", "ep"), NODE, None),
        P(("groups", "ep"), None),
        P(NODE, None, None),
        P(("groups", "ep"), None),
        P(("groups", "ep"), None),
        P(),
        P("ep", None, NODE),
        P("ep", None, NODE),
        P("ep", NODE, None),
    )
    return jax.shard_map(
        per_device,
        mesh=torus,
        in_specs=placed,
        out_specs=(P(("groups", "ep"), NODE), P(("groups", "ep"), NODE)),
        check_vma=False,
    )
```

profile of v0, /device:TPU:40, one launch (start us, length us, event | category | flops | bytes accessed | tf_op | source)
XLA Modules:
  0.0 229.9 jit_solution(9567413395786165670)
XLA Ops:
  7.2 0.1 all-gather.8.cloned.1.call-start
  7.3 0.8 fusion.60
  8.1 0.8 copy.89
  8.9 0.1 copy.93
  9.0 0.1 reshape.172
  9.1 1.9 gather_fusion.3
  11.1 0.1 reshape.181
  11.2 0.1 reshape.143
  11.3 0.1 reshape.196
  11.4 1.4 scatter_custom_fusion.1
  12.8 1.4 scatter_custom_fusion
  14.3 0.1 broadcast_in_dim.77
  14.4 2.1 gather_fusion
  16.5 0.1 broadcast_select_fusion
  16.6 47.6 %all_to_all.15 = bf16[16,1,24,512]{3,2,1,0:T(8,128)(2,1)} all-to-all(bf16[16,1,24,512]{3,2,1,0:T(8,128)(2,1)S(1)} %broadcast_select_fusion), channel_id=1, replica_groups=mesh['groups'=2,'ep'=16,'node_0'=4,'node_1'=2] {'ep'}, dimensions={0} | all-to-all | bytes 786432 | tf_op jit(solution)/shard_map/all_to_all | solution.py:112
  64.3 0.1 all-gather.10.cloned.1.call-start
  64.3 28.0 %all-gather.8.cloned.1.call-done = bf16[64,1,24,512]{3,2,1,0:T(8,128)(2,1)} async-done(((bf16[16,1,24,512]{3,2,1,0:T(8,128)(2,1)}), bf16[64,1,24,512]{3,2,1,0:T(8,128)(2,1)}) %all-gather.8.cloned.1.call-update) | async-done | bytes 1572880 | tf_op jit(solution)/shard_map/all_gather | solution.py:23
  92.4 0.1 all-gather.6.cloned.1.call-start
  92.5 0.8 copy.87
  93.3 21.8 %all-gather.10.cloned.1.call-done = bf16[8,16,1,24,512]{4,3,2,1,0:T(8,128)(2,1)} async-done(((bf16[4,16,1,24,512]{4,3,2,1,0:T(8,128)(2,1)}), bf16[8,16,1,24,512]{4,3,2,1,0:T(8,128)(2,1)}) %all-gather.10.cloned.1.call-update) | async-done | bytes 3145744 | tf_op jit(solution)/shard_map/all_gather | solution.py:23
  115.2 2.1 copy.96
  117.3 3.5 %copy.97 = bf16[16,1,24,8,512]{4,3,2,0,1:T(8,128)(2,1)} copy(bf16[16,1,24,8,512]{4,2,0,3,1:T(8,128)(2,1)S(1)} %bitcast.165) | data formatting | bytes 6291456 | tf_op jit(solution)/shard_map/transpose | solution.py:15
  120.8 5.9 %reshape.146 = bf16[16,24,4096]{2,1,0:T(8,128)(2,1)} reshape(bf16[16,1,24,8,512]{4,3,2,0,1:T(8,128)(2,1)} %copy.97) | data formatting | bytes 6291456 | tf_op jit(solution)/shard_map/reshape.8
  126.7 3.5 %fusion.18 = f32[16,1,24,256]{3,2,0,1:T(8,128)S(1)} fusion(bf16[16,24,4096]{2,1,0:T(8,128)(2,1)} %reshape.146, bf16[1,4096,256]{2,1,0:T(8,128)(2,1)} %param.17), kind=kOutput, calls=%fused_computation.32 | convolution fusion | flops 805306368 | bytes 5636096 | tf_op jit(solution)/shard_map/sjcd,jdf->sjcf/dot_general | solution.py:114
  130.2 7.8 %convolution_convert_fusion = bf16[16,24,4096]{2,1,0:T(8,128)(2,1)} fusion(bf16[1,256,4096]{2,1,0:T(8,128)(2,1)S(1)} %copy-done, bf16[16,24,4096]{2,1,0:T(8,128)(2,1)} %reshape.146, bf16[1,4096,256]{2,1,0:T(8,128)(2,1)} %param.18, f32[16,1,24,256]{3,2,0,1:T(8,128)S(1)} %fusion.18), kind=kOutput, calls=%fused_computation.23 | convolution fusion | flops 1612775424 | bytes 10878976 | tf_op jit(solution)/shard_map/sjcf,jfd->sjcd/dot_general | solution.py:117
  138.0 2.2 copy.175
  140.2 42.6 %all_to_all.16 = bf16[8,16,1,24,512]{4,3,1,2,0:T(8,128)(2,1)} all-to-all(bf16[8,16,1,24,512]{4,3,1,2,0:T(8,128)(2,1)S(1)} %bitcast.166), channel_id=1, replica_groups=mesh['groups'=2,'ep'=16,'node_0'=4,'node_1'=2] {'node_0','node_1'}, dimensions={0} | all-to-all | bytes 6291456 | tf_op jit(solution)/shard_map/all_to_all | solution.py:41
  182.8 3.2 %reduce_sum.33 = bf16[16,24,512]{2,1,0:T(8,128)(2,1)} reduce(bf16[8,16,1,24,512]{4,3,1,2,0:T(8,128)(2,1)} %all_to_all.16, bf16[]{:T(256)} %constant.95.clone.1), dimensions={0,2}, to_apply=%region_9.10 | reduce | flops 1376256 | bytes 3538946 | tf_op jit(solution)/shard_map/reduce_sum | solution.py:42
  186.0 12.4 %all-to-all-start.2 = ((bf16[16,1,24,512]{3,2,1,0:T(8,128)(2,1)}), bf16[16,1,24,512]{3,2,1,0:T(8,128)(2,1)S(1)}, u32[]{:S(2)}, u32[]{:S(2)}) async-start(bf16[16,1,24,512]{3,2,1,0:T(8,128)(2,1)} %bitcast.33), calls=%async_computation.2 | async-start | bytes 786432 | tf_op jit(solution)/shard_map/all_to_all | solution.py:121
  198.4 0.1 reshape.166
  198.5 0.2 fusion.37
  198.7 2.0 gather_fusion.2
  200.7 0.1 reshape.175
  200.8 0.1 select_reduce_fusion
  200.9 0.1 multiply_divide_fusion
  201.0 0.3 slice_reduce_fusion.7
  201.4 11.4 %conditional.1 = (f32[128,8]{0,1:T(8,128)S(1)}, f32[128,8,512]{2,0,1:T(8,128)S(1)}) conditional(s32[]{:T(128)} %convert_element_type.41, () %tuple.16, (s32[]{:T(128)}, bf16[128,8,576]{0,2,1:T(8,128)(2,1)}, bf16[2048,576]{1,0:T(8,128)(2,1)}) %tuple.17), branch_computations={%region_0.0_spmd, %region_1.4_spmd} | conditional | flops 4590926848 | bytes 43410480 | solution.py:75
  201.4 0.2 iota_compare_fusion
  201.6 6.1 %fusion = (f32[128,8]{0,1:T(8,128)S(1)}, f32[128,8,2048]{2,0,1:T(8,128)S(1)}) fusion(pred[128,2048]{1,0:T(8,128)(4,1)S(1)} %iota_compare_fusion, bf16[128,8,576]{0,2,1:T(8,128)(2,1)} %get-tuple-element.16, bf16[2048,576]{1,0:T(8,128)(2,1)} %get-tuple-element.8), kind=kOutput, calls=%fused_computation.8 | convolution fusion | flops 2422209536 | bytes 12193792 | tf_op jit(solution)/shard_map/cond/branch_1_fun/qhc,kc->qhk/dot_general | solution.py:50
  207.7 2.5 %fusion.2 = f32[128,8]{0,1:T(8,128)S(1)} fusion(f32[128,8,2048]{2,0,1:T(8,128)S(1)} %get-tuple-element.38, f32[128,8]{0,1:T(8,128)S(1)} %broadcast_maximum_fusion, pred[128,2048]{1,0:T(8,128)(4,1)S(1)} %iota_compare_fusion), kind=kLoop, calls=%fused_computation.10 | loop fusion | flops 10484736 | bytes 8658944 | tf_op jit(solution)/shard_map/cond/branch_1_fun/reduce_sum | solution.py:54
  210.3 2.5 %fusion.3 = f32[128,8,512]{2,0,1:T(8,128)S(1)} fusion(f32[128,8,2048]{2,0,1:T(8,128)S(1)} %get-tuple-element.38, f32[128,8]{0,1:T(8,128)S(1)} %broadcast_maximum_fusion, pred[128,2048]{1,0:T(8,128)(4,1)S(1)} %iota_compare_fusion, bf16[2048,576]{1,0:T(8,128)(2,1)S(1)} %copy-done.4), kind=kOutput, calls=%fused_computation.11 | convolution fusion | flops 2157969408 | bytes 12849152 | tf_op jit(solution)/shard_map/cond/branch_1_fun/qhk,kc->qhc/dot_general | solution.py:56
  212.8 1.9 convolution_convert_fusion.1
  214.7 0.9 copy.107
  215.5 5.6 %all-to-all-done.2 = bf16[16,1,24,512]{3,2,1,0:T(8,128)(2,1)S(1)} async-done(((bf16[16,1,24,512]{3,2,1,0:T(8,128)(2,1)}), bf16[16,1,24,512]{3,2,1,0:T(8,128)(2,1)S(1)}, u32[]{:S(2)}, u32[]{:S(2)}) %all-to-all-start.2) | async-done | bytes 393248 | tf_op jit(solution)/shard_map/all_to_all | solution.py:121
  221.2 0.1 bitcast_convert_fusion
  221.3 1.0 gather_fusion.1
  222.3 0.4 fusion.66
  222.6 0.7 fusion.46
  (29 shorter events, 0.4 us)
Async XLA Ops:
  7.2 123.0 %copy-start = (bf16[1,256,4096]{2,1,0:T(8,128)(2,1)S(1)}, bf16[1,256,4096]{2,1,0:T(8,128)(2,1)}, u32[]{:S(2)}) copy-start(bf16[1,256,4096]{2,1,0:T(8,128)(2,1)} %param.19) | copy-start | bytes 6291460
  7.2 85.1 %all-gather.8.cloned.1.call-start = ((), (), s32[]{:S(2)}) async-start(), calls=%async_computation.4 | async-start | bytes 1966080 | tf_op jit(solution)/shard_map/all_gather | solution.py:23
  9.1 5.2 %copy-start.1 = (bf16[32,4096]{1,0:T(8,128)(2,1)S(1)}, bf16[32,4096]{1,0:T(8,128)(2,1)}, u32[]{:S(2)}) copy-start(bf16[32,4096]{1,0:T(8,128)(2,1)} %param.14) | copy-start | bytes 786436
  14.4 78.1 %copy-start.2 = (bf16[128,576]{0,1:T(8,128)(2,1)S(1)}, bf16[128,576]{0,1:T(8,128)(2,1)}, u32[]{:S(2)}) copy-start(bf16[128,576]{0,1:T(8,128)(2,1)} %param.12) | copy-start | bytes 442372
  64.3 50.9 %all-gather.10.cloned.1.call-start = ((), (), s32[]{:S(2)}) async-start(), calls=%async_computation.5 | async-start | bytes 4718592 | tf_op jit(solution)/shard_map/all_gather | solution.py:23
  92.4 109.0 %all-gather.6.cloned.1.call-start = ((), (), s32[]{:S(2)}) async-start(), calls=%async_computation.3 | async-start | bytes 2785280 | tf_op jit(solution)/shard_map/all_gather | solution.py:74
  182.8 15.7 %copy-start.3 = (bf16[4096,16]{0,1:T(8,128)(2,1)S(1)}, bf16[4096,16]{0,1:T(8,128)(2,1)}, u32[]{:S(2)}) copy-start(bf16[4096,16]{0,1:T(8,128)(2,1)} %param.16) | copy-start | bytes 393220
  186.0 35.1 %all-to-all-start.2 = ((bf16[16,1,24,512]{3,2,1,0:T(8,128)(2,1)}), bf16[16,1,24,512]{3,2,1,0:T(8,128)(2,1)S(1)}, u32[]{:S(2)}, u32[]{:S(2)}) async-start(bf16[16,1,24,512]{3,2,1,0:T(8,128)(2,1)} %bitcast.33), calls=%async_computation.2 | async-start | bytes 786432 | tf_op jit(solution)/shard_map/all_to_all | solution.py:121
  207.7 2.5 %copy-start.4 = (bf16[2048,576]{1,0:T(8,128)(2,1)S(1)}, bf16[2048,576]{1,0:T(8,128)(2,1)}, u32[]{:S(2)}) copy-start(bf16[2048,576]{1,0:T(8,128)(2,1)} %get-tuple-element.8) | copy-start | bytes 7077892 | tf_op jit(solution)/shard_map/cond
Sparse Core Ops, SparseCore 0:
  64.4 27.8 all-gather.7
  94.1 20.9 all-gather.9
  117.6 73.8 all-gather.5
where the time goes:
time: 230 us
  blocking collectives  90.2 us (39%)
  waiting for transfers between devices  55.6 us (24%)
  local copies, waits for them, and re-layouts  27.3 us (12%)
  matrix products  22 us (10%)
  between operations  14 us (6%)
  starting transfers between devices  12.5 us (5%)
  other arithmetic  8.1 us (4%)
    all_gather x2, waiting for transfers between devices, all_blocks(): tiles = lax.all_gather(tiles, axes[k])  49.8 us
    all_to_all x1, blocking collectives, per_device(): lax.all_to_all(outgoing, 'ep', split_axis=0, concat_axis=0, tiled=True)  47.6 us
    all_to_all x1, blocking collectives, sent_and_summed(): lax.all_to_all(tiles, axis, split_axis=0, concat_axis=0, tiled=True)  42.6 us
    all_to_all x1, starting transfers between devices, per_device(): lax.all_to_all(summed.astype(jnp.bfloat16), 'ep', split_axis=0, concat_ax...  12.4 us
    dot_general x1, matrix products, per_device(): jnp.einsum('sjcf,jfd->sjcd', hidden, w_down, preferred_element_type=jnp.f...  7.77 us
    dot_general x1, matrix products, attend_block(): jnp.einsum('qhc,kc->qhk', queries, piece, preferred_element_type=jnp.floa...  6.09 us
    another operation x1, local copies, waits for them, and re-layouts  5.89 us
    all_to_all x1, waiting for transfers between devices, per_device(): lax.all_to_all(summed.astype(jnp.bfloat16), 'ep', split_axis=0, concat_ax...  5.63 us
  transfers between devices with their start and end apart: 4, of which 3 were waited for; matrix products, arithmetic and copies ran while one was open for 20% of the time, Pallas kernels for 0%

commit v1 on v0

v1 whole, which is shorter than its diff:
```python
import functools

import jax
import jax.numpy as jnp
from jax import lax
from jax.experimental import pallas as pl
from jax.experimental.pallas import tpu as pltpu
from jax.sharding import Mesh
from jax.sharding import PartitionSpec as P

NODE = ("node_0", "node_1")
ROUTED_SCALE = 2.5
NEGATIVE = -1e30
MESH = pl.DeviceIdType.MESH
BF = jnp.bfloat16
F32 = jnp.float32
NEAR = 9


def slots_of(d):
    return (2 * d - 1, 2 * d + 1) if d < 8 else (15, 16)


def kernel(
    scale,
    tok, lat, q_hbm, wg_hbm, wu_hbm, wd_hbm, wv_hbm,
    out_a, out_m,
    X, LT, Q, WG, WU, WD, WV, S, SE, MX, CTX, HID, O, DB, XS, XR, ZS, ZR, FS, FR,
    z_s, z_r, x_s, x_r, d_s, d_r, l_s, l_r, lx_s, lx_r, ld_s, ld_r,
    rd_s, rd_r, rx_s, rx_r, rz_s, rz_r, f_s, f_r, loc,
):
    n_ep = lax.axis_size("ep")
    n_x = lax.axis_size("node_0")
    z = lax.axis_index("ep")
    c = lax.axis_index("node_0")
    k = lax.axis_index("node_1")
    p = lax.rem(c, 2)
    above = {"ep": lax.rem(z + 1, n_ep)}
    below = {"ep": lax.rem(z + n_ep - 1, n_ep)}
    right = {"node_0": lax.rem(c + 1, n_x)}
    left = {"node_0": lax.rem(c + n_x - 1, n_x)}
    across = {"node_0": lax.rem(c + 2, n_x)}
    partner = {"node_1": 1 - k}
    give = {"node_0": lax.rem(c + n_x + 1 - 2 * k, n_x)}
    send_back = {"node_0": lax.rem(c + n_x - 1 + 2 * k, n_x)}
    tile = p * 2 + k

    barrier = pltpu.get_barrier_semaphore()
    for peer in (above, below, right, left, across, partner):
        pl.semaphore_signal(barrier, inc=1, device_id=peer, device_id_type=MESH)

    local = [pltpu.make_async_copy(q_hbm, Q, loc.at[0])]
    local.append(pltpu.make_async_copy(wg_hbm.at[0], WG, loc.at[1]))
    local.append(pltpu.make_async_copy(wu_hbm.at[0], WU, loc.at[2]))
    local.append(pltpu.make_async_copy(wv_hbm, WV, loc.at[3]))
    for n in range(8):
        local.append(
            pltpu.make_async_copy(
                wd_hbm.at[0, :, n * 512 : (n + 1) * 512], WD.at[n], loc.at[4 + n]
            )
        )

    def remote(src, dst, s, r, peer):
        return pltpu.make_async_remote_copy(
            src_ref=src, dst_ref=dst, send_sem=s, recv_sem=r, device_id=peer, device_id_type=MESH
        )

    own_x = (p, p + 2)
    sent = []

    def go(copy):
        copy.start()
        sent.append(copy)

    def z_copy(d, way, h):
        dst = 2 * d - 1 + way
        src = tok.at[2 * own_x[h] + k] if d == 1 else X.at[own_x[h], k, dst - 2]
        return remote(
            src, X.at[own_x[h], k, dst], z_s.at[way, h, d - 1], z_r.at[way, h, d - 1],
            below if way else above,
        )

    def l_copy(d, way):
        dst = 2 * d - 1 + way
        src = lat.at[pl.ds(pl.multiple_of(tile * 32, 32), 32)] if d == 1 else LT.at[p, k, dst - 2]
        return remote(
            src, LT.at[p, k, dst], l_s.at[way, d - 1], l_r.at[way, d - 1], below if way else above
        )

    def x_copy(d, h):
        a, b = slots_of(d)
        ref = X.at[own_x[h], k, a:b]
        return remote(ref, ref, x_s.at[h, d - 1], x_r.at[h, d - 1], give)

    def x_wait(d, h):
        a, b = slots_of(d)
        ref = X.at[1 - p + 2 * h, k, a:b]
        remote(ref, ref, x_s.at[h, d - 1], x_r.at[h, d - 1], give).wait_recv()

    def lx_copy(d):
        a, b = slots_of(d)
        ref = LT.at[p, k, a:b]
        return remote(ref, ref, lx_s.at[d - 1], lx_r.at[d - 1], give)

    def lx_wait(d):
        a, b = slots_of(d)
        ref = LT.at[1 - p, k, a:b]
        remote(ref, ref, lx_s.at[d - 1], lx_r.at[d - 1], give).wait_recv()

    def d_copy(d, core):
        a, b = slots_of(d)
        ref = X.at[:, core, a:b]
        return remote(ref, ref, d_s.at[d - 1], d_r.at[d - 1], partner)

    def ld_copy(d, core):
        a, b = slots_of(d)
        ref = LT.at[:, core, a:b]
        return remote(ref, ref, ld_s.at[d - 1], ld_r.at[d - 1], partner)

    def ways(d):
        return (0, 1) if d < 8 else (0,)

    def keys_of(d):
        a, b = slots_of(d)
        return LT[:, :, a:b].reshape(128 * (b - a), 640)

    def scores_first():
        keys = lat[...][:, :576]

        def body(t, carry):
            rows = pl.ds(pl.multiple_of(t * 256, 256), 256)
            s = lax.dot_general(Q[rows], keys, (((1,), (1,)), ((), ())), preferred_element_type=F32)
            query = t * 32 + lax.broadcasted_iota(jnp.int32, s.shape, 0) // 8
            key = lax.broadcasted_iota(jnp.int32, s.shape, 1)
            s = jnp.where(key <= query, s, NEGATIVE)
            SE[0, rows] = s
            MX[rows] = s
            return carry

        lax.fori_loop(0, 4, body, 0)

    def scores(d):
        a, b = slots_of(d)
        keys = keys_of(d)[:, :576]
        size = 128 * (b - a)
        low = jnp.where(z >= d, 0.0, NEGATIVE).astype(F32)
        high = jnp.where(z + d >= n_ep, 0.0, NEGATIVE).astype(F32)
        if d < 8:
            at = lax.broadcasted_iota(jnp.int32, (1, size), 1)
            bias = jnp.where((at // 32) % 2 == 0, low, high)
        else:
            bias = low

        def body(t, carry):
            rows = pl.ds(pl.multiple_of(t * 256, 256), 256)
            s = lax.dot_general(Q[rows], keys, (((1,), (1,)), ((), ())), preferred_element_type=F32)
            s = s + bias
            if d < 8:
                S[d - 1, rows] = s
                MX[rows] = jnp.maximum(MX[rows], jnp.maximum(s[:, :128], s[:, 128:]))
            else:
                SE[1, rows] = s
                MX[rows] = jnp.maximum(MX[rows], s)
            return carry

        lax.fori_loop(0, 4, body, 0)

    def context(t):
        rows = pl.ds(t * 256, 256)
        top = jnp.max(MX[rows], axis=1, keepdims=True)
        s = SE[0, rows]
        e = jnp.exp((s - top) * scale)
        total = e
        acc = jnp.dot(e.astype(BF), lat[...][:, :512], preferred_element_type=F32)
        for d in range(1, 9):
            s = S[d - 1, rows] if d < 8 else SE[1, rows]
            e = jnp.exp((s - top) * scale)
            total = total + (e[:, :128] + e[:, 128:] if d < 8 else e)
            acc = acc + jnp.dot(e.astype(BF), keys_of(d)[:, :512], preferred_element_type=F32)
        acc = acc / jnp.sum(total, axis=1, keepdims=True)
        for n in range(4):
            CTX[n, rows] = acc[:, n * 128 : (n + 1) * 128]

    def values():
        for h in range(8):
            part = jnp.concatenate(
                [CTX[n, pl.ds(h, 128, stride=8), :].astype(BF) for n in range(4)], axis=1
            )
            out_a[:, h * 128 : (h + 1) * 128] = jnp.dot(
                part, WV[h], preferred_element_type=F32
            ).astype(BF)

    def expert_in(a, b):
        rows = 32 * (b - a)
        lhs = jnp.concatenate([X[n // 2, n % 2, a:b].reshape(rows, 512) for n in range(8)], axis=1)
        gate = jnp.dot(lhs, WG[...], preferred_element_type=F32)
        upward = jnp.dot(lhs, WU[...], preferred_element_type=F32)
        hidden = gate / (1.0 + jnp.exp(-gate)) * upward
        HID[a * 32 : b * 32] = hidden.astype(BF)

    def gates_of(a, b):
        parts = []
        if a == 0:
            parts.append(lat[0:32, 512:640])
            a = 1
        parts.append(LT[p, k, a:b, :, 512:640].reshape(32 * (b - a), 128))
        both = jnp.concatenate(parts, axis=0).astype(F32)
        lane = lax.broadcasted_iota(jnp.int32, both.shape, 1)
        mine = (lane == 64 + z) | (lane == 80 + z)
        return jnp.sum(jnp.where(mine, both, 0.0), axis=1, keepdims=True)

    def expert_out(a, b, core):
        g = gates_of(a, b)
        hidden = HID[a * 32 : b * 32]

        def body(x, carry):
            o = jnp.dot(hidden, WD[2 * x + core], preferred_element_type=F32) * g
            O[x, core, a:b] = o.astype(BF).reshape(b - a, 32, 512)
            return carry

        lax.fori_loop(0, 4, body, 0)

    GROUPS = ((0, NEAR), (9, 11), (11, 13), (13, 15), (15, 16))

    def rd_copy(i):
        a, b = GROUPS[i]
        return remote(O.at[:, 1 - k, a:b], DB.at[:, a:b], rd_s.at[i], rd_r.at[i], partner)

    def rx_copy(i):
        a, b = GROUPS[i]
        return remote(XS.at[:, a:b], XR.at[:, a:b], rx_s.at[i], rx_r.at[i], send_back)

    def pass_on(i):
        a, b = GROUPS[i]
        rd_copy(i).wait_recv()
        for h in range(2):
            x = 1 - p + 2 * h
            XS[h, a:b] = (O[x, k, a:b].astype(F32) + DB[x, a:b].astype(F32)).astype(BF)
        go(rx_copy(i))

    def summed(h, slot):
        x = own_x[h]
        return O[x, k, slot].astype(F32) + DB[x, slot].astype(F32) + XR[h, slot].astype(F32)

    def rz_copy(j, way, h):
        return remote(
            ZS.at[way, j - 1, h], ZR.at[way, j - 1, h],
            rz_s.at[way, h, j - 1], rz_r.at[way, h, j - 1], below if way else above,
        )

    for copy in local:
        copy.start()
    pl.semaphore_wait(barrier, 6)
    for h in range(2):
        for way in ways(1):
            go(z_copy(1, way, h))
    for way in ways(1):
        go(l_copy(1, way))
    for n in range(8):
        X[n // 2, n % 2, 0] = tok[n]
    local[0].wait()
    scores_first()

    for d in range(1, 9):
        for h in range(2):
            for way in ways(d):
                z_copy(d, way, h).wait_recv()
                if way in ways(d + 1) and d < 8:
                    go(z_copy(d + 1, way, h))
            go(x_copy(d, h))
        for way in ways(d):
            l_copy(d, way).wait_recv()
            if way in ways(d + 1) and d < 8:
                go(l_copy(d + 1, way))
        go(lx_copy(d))
        if d >= 2:
            for h in range(2):
                x_wait(d - 1, h)
            go(d_copy(d - 1, k))
            lx_wait(d - 1)
            go(ld_copy(d - 1, k))
        if d >= 3:
            d_copy(d - 2, 1 - k).wait_recv()
            ld_copy(d - 2, 1 - k).wait_recv()
            scores(d - 2)
        if d == 6:
            for copy in local[1:3]:
                copy.wait()
            expert_in(0, NEAR)
        if d == 7:
            for copy in local[3:]:
                copy.wait()
            expert_out(0, NEAR, 1 - k)
            go(rd_copy(0))
            expert_out(0, NEAR, k)
    for h in range(2):
        x_wait(8, h)
    go(d_copy(8, k))
    lx_wait(8)
    go(ld_copy(8, k))
    for d in (7, 8):
        d_copy(d, 1 - k).wait_recv()
        ld_copy(d, 1 - k).wait_recv()

    expert_in(NEAR, 16)
    expert_out(NEAR, 16, 1 - k)
    for i in (4, 3, 2, 1):
        go(rd_copy(i))
    expert_out(NEAR, 16, k)
    for i in (4, 3, 2, 1, 0):
        pass_on(i)

    ready = set()
    for j in range(1, 9):
        for way in (0, 1):
            if way and j == 8:
                continue
            dist = 8 - j if way else 9 - j
            slot = 2 * dist - 1 if (way or dist == 8) else 2 * dist
            i = [n for n, (a, b) in enumerate(GROUPS) if a <= slot < b][0]
            if i not in ready:
                rx_copy(i).wait_recv()
                ready.add(i)
            for h in range(2):
                total = summed(h, slot)
                if j > 1:
                    rz_copy(j - 1, way, h).wait_recv()
                    total = total + ZR[way, j - 2, h].astype(F32)
                ZS[way, j - 1, h] = total.astype(BF)
                go(rz_copy(j, way, h))
        if j == 1:
            scores(7)
        if j == 2:
            scores(8)
        if 3 <= j <= 6:
            context(j - 3)
        if j == 7:
            values()

    mine = lax.div(c, 2)
    kept = []
    for h in range(2):
        rz_copy(8, 0, h).wait_recv()
        rz_copy(7, 1, h).wait_recv()
        kept.append(summed(h, 0) + ZR[0, 7, h].astype(F32) + ZR[1, 6, h].astype(F32))
    FS[...] = jnp.where(mine == 0, kept[1], kept[0]).astype(BF)
    last = remote(FS, FR, f_s.at[0], f_r.at[0], across)
    go(last)
    last.wait_recv()
    out_m[...] = (jnp.where(mine == 0, kept[0], kept[1]) + FR[...].astype(F32)).astype(BF)
    for copy in sent:
        copy.wait_send()


def per_device(queries, latent_kv, w_value, moe_tokens, routes, router, w_gate, w_up, w_down):
    seq_dev, heads_dev, width = queries.shape
    latent_width, value_width = w_value.shape[1:]
    tokens_dev, model_width = moe_tokens.shape
    experts = router.shape[1]
    scale = (value_width + width - latent_width) ** (-0.5)

    affinity = jax.nn.sigmoid(jnp.dot(moe_tokens, router, preferred_element_type=F32))
    expert_range = lax.iota(jnp.int32, experts)
    member = jnp.any(routes[:, :, None] == expert_range[None, None, :], axis=1)
    chosen = jnp.where(member, affinity, 0.0)
    gates = ROUTED_SCALE * chosen / jnp.sum(chosen, axis=1, keepdims=True)
    high = gates.astype(BF)
    low = (gates - high.astype(F32)).astype(BF)
    extra = jnp.concatenate([high, low, jnp.zeros((tokens_dev, 32), BF)], axis=1)
    lat = jnp.concatenate([latent_kv, jnp.tile(extra, (seq_dev // tokens_dev, 1))], axis=1)

    tok = moe_tokens.reshape(tokens_dev, 8, 512).transpose(1, 0, 2)
    rows = seq_dev * heads_dev
    dma = pltpu.SemaphoreType.DMA
    vmem = pl.BlockSpec(memory_space=pltpu.VMEM)
    hbm = pl.BlockSpec(memory_space=pl.ANY)
    return pl.pallas_call(
        functools.partial(kernel, scale),
        out_shape=(
            jax.ShapeDtypeStruct((seq_dev, heads_dev * value_width), BF),
            jax.ShapeDtypeStruct((tokens_dev, 512), BF),
        ),
        in_specs=[vmem, vmem] + [hbm] * 5,
        out_specs=(vmem, vmem),
        scratch_shapes=[
            pltpu.VMEM((4, 2, 16, 32, 512), BF),
            pltpu.VMEM((2, 2, 16, 32, 640), BF),
            pltpu.VMEM((rows, width), BF),
            pltpu.VMEM((model_width, 256), BF),
            pltpu.VMEM((model_width, 256), BF),
            pltpu.VMEM((8, 256, 512), BF),
            pltpu.VMEM((heads_dev, latent_width, value_width), BF),
            pltpu.VMEM((7, rows, 256), F32),
            pltpu.VMEM((2, rows, 128), F32),
            pltpu.VMEM((rows, 128), F32),
            pltpu.VMEM((4, rows, 128), F32),
            pltpu.VMEM((512, 256), BF),
            pltpu.VMEM((4, 2, 16, 32, 512), BF),
            pltpu.VMEM((4, 16, 32, 512), BF),
            pltpu.VMEM((2, 16, 32, 512), BF),
            pltpu.VMEM((2, 16, 32, 512), BF),
            pltpu.VMEM((2, 8, 2, 32, 512), BF),
            pltpu.VMEM((2, 8, 2, 32, 512), BF),
            pltpu.VMEM((32, 512), BF),
            pltpu.VMEM((32, 512), BF),
            dma((2, 2, 8)), dma((2, 2, 8)),
            dma((2, 8)), dma((2, 8)),
            dma((8,)), dma((8,)),
            dma((2, 8)), dma((2, 8)),
            dma((8,)), dma((8,)),
            dma((8,)), dma((8,)),
            dma((5,)), dma((5,)),
            dma((5,)), dma((5,)),
            dma((2, 2, 8)), dma((2, 2, 8)),
            dma((1,)), dma((1,)),
            dma((12,)),
        ],
        compiler_params=pltpu.CompilerParams(
            collective_id=0, has_side_effects=True, vmem_limit_bytes=60 * 1024 * 1024
        ),
    )(tok, lat, queries.reshape(rows, width), w_gate, w_up, w_down, w_value)


def solution(mesh):
    torus = Mesh(
        mesh.devices.reshape(mesh.shape["groups"], mesh.shape["ep"], mesh.shape["node"] // 2, 2),
        ("groups", "ep", "node_0", "node_1"),
    )
    placed = (
        P(("groups", "ep"), NODE, None),
        P(("groups", "ep"), None),
        P(NODE, None, None),
        P(("groups", "ep"), None),
        P(("groups", "ep"), None),
        P(),
        P("ep", None, NODE),
        P("ep", None, NODE),
        P("ep", NODE, None),
    )
    return jax.shard_map(
        per_device,
        mesh=torus,
        in_specs=placed,
        out_specs=(P(("groups", "ep"), NODE), P(("groups", "ep"), NODE)),
        check_vma=False,
    )
```

time: 230 us -> 110 us (0.48)
  Pallas kernels: 0 us -> 98.6 us
  blocking collectives: 90.2 us -> 0 us
  waiting for transfers between devices: 55.6 us -> 0 us
  matrix products: 22 us -> 1.16 us
  local copies, waits for them, and re-layouts: 27.3 us -> 8.13 us
  between operations: 14 us -> 0.69 us
  starting transfers between devices: 12.5 us -> 0 us
  other arithmetic: 8.1 us -> 1.64 us
    pallas_call x0 -> x1, Pallas kernels: none -> 98.6 us  [per_device(): pl.pallas_call(functools.partial(kernel, scale), out_shape=(jax.ShapeDtyp...]
    all_to_all x2 -> x0, blocking collectives: 90.2 us -> none  [the longest x1 47.6 us: per_device(): lax.all_to_all(outgoing, 'ep', split_axis=0, concat_axis=0, tiled=True)]
    all_gather x3 -> x0, waiting for transfers between devices: 49.8 us -> none  [the longest x2 49.8 us: all_blocks(): tiles = lax.all_gather(tiles, axes[k])]
    dot_general x6 -> x1, matrix products: 22 us -> 1.16 us  [per_device(): jnp.dot(moe_tokens, router, preferred_element_type=F32)]
    all_to_all x1 -> x0, starting transfers between devices: 12.4 us -> none  [per_device(): lax.all_to_all(summed.astype(jnp.bfloat16), 'ep', split_axis=0, concat_ax...]
    gather x7 -> x0, local copies, waits for them, and re-layouts: 7.27 us -> none  [the longest x3 2.2 us: per_device(): chosen = jnp.take_along_axis(affinity, routes, axis=1)]
    another operation x1, local copies, waits for them, and re-layouts: 5.89 us -> 0.01 us  [per_device(): jnp.tile(extra, (seq_dev // tokens_dev, 1))]
    reduce_sum x3 -> x0, other arithmetic: 5.87 us -> none  [the longest x1 3.23 us: sent_and_summed(): return arrived.astype(jnp.float32).sum(axis=0)]
  transfers between devices with their start and end apart: 4 -> 0, of which waited for: 3 -> 0; matrix products, arithmetic and copies ran while one was open for 20% -> 0% of each run, Pallas kernels for 0% -> 0%
where the time goes in v1:
time: 110 us
  Pallas kernels  98.6 us (90%)
  local copies, waits for them, and re-layouts  8.13 us (7%)
  other arithmetic  1.64 us (1%)
  matrix products  1.16 us (1%)
    pallas_call x1, Pallas kernels, per_device(): pl.pallas_call(functools.partial(kernel, scale), out_shape=(jax.ShapeDtyp...  98.6 us
    unnamed x8, local copies, waits for them, and re-layouts  6.19 us

profile of v1, /device:TPU:40, one launch (start us, length us, event | category | flops | bytes accessed | tf_op | source)
XLA Modules:
  0.0 110.2 jit_solution(474395962421920057)
XLA Ops:
  0.6 0.0 copy-start
  0.6 0.0 copy-start.1
  0.7 0.1 pad.4.clone
  0.7 0.8 fusion.4
  1.5 0.0 copy-done
  1.5 1.2 %fusion.6 = (f32[32]{0:T(128)S(1)}, f32[32,16]{0,1:T(8,128)S(1)}) fusion(pred[32,16]{0,1:T(8,128)(4,1)S(1)} %fusion.4, bf16[32,4096]{1,0:T(8,128)(2,1)} %param.12, bf16[4096,16]{0,1:T(8,128)(2,1)S(1)} %copy-done), kind=kOutput, calls=%fused_computation.13 | convolution fusion | flops 4196832 | bytes 395904 | tf_op jit(solution)/shard_map/dot_general | solution.py:362
  2.7 0.1 copy.23
  2.8 0.1 copy.24
  2.9 0.1 maximum_maximum_fusion
  3.0 1.1 copy.25
  4.1 0.8 pad_maximum_fusion.lat
  4.8 1.7 %copy.29 = bf16[4,8,8,512]{3,2,0,1:T(8,128)(2,1)} copy(bf16[4,8,8,512]{3,2,1,0:T(8,128)(2,1)} %bitcast.13) | data formatting | bytes 524288 | tf_op jit(solution)/shard_map/reshape | solution.py:372
  6.5 0.0 copy-done.1
  6.5 2.1 %copy.26 = bf16[128,8,576]{2,1,0:T(8,128)(2,1)} copy(bf16[128,8,576]{0,2,1:T(8,128)(2,1)S(1)} %copy-done.1) | data formatting | bytes 2359296 | tf_op args[0]
  8.6 98.6 %shard_map.104 = (bf16[128,1024]{1,0:T(8,128)(2,1)}, bf16[32,512]{1,0:T(8,128)(2,1)}) custom-call(bf16[8,32,512]{2,1,0:T(8,128)(2,1)} %bitcast.12, bf16[128,640]{1,0:T(8,128)(2,1)} %pad_maximum_fusion.lat, bf16[1024,576]{1,0:T(8,128)(2,1)} %bitcast.11, bf16[1,4096,256]{2,1,0:T(8,128)(2,1)} %wg_hbm.1, bf16[1,4096,256]{2,1,0:T(8,128)(2,1)} %wu_hbm.1, ...), custom_call_target="tpu_custom_call" | custom-call | tf_op jit(solution)/shard_map/pallas_call | solution.py:377
  107.1 1.7 %copy.32 = bf16[128,1024]{1,0:T(8,128)(2,1)} copy(bf16[128,1024]{1,0:T(8,128)(2,1)} %get-tuple-element.8) | data formatting | bytes 524288
  108.8 1.4 %copy.33 = bf16[32,512]{1,0:T(8,128)(2,1)} copy(bf16[32,512]{1,0:T(8,128)(2,1)} %get-tuple-element.9) | data formatting | bytes 65536
  (3 shorter events, 0.0 us)
Async XLA Ops:
  0.6 0.9 copy-start
  0.6 5.9 %copy-start.1 = (bf16[128,8,576]{0,2,1:T(8,128)(2,1)S(1)}, bf16[128,8,576]{0,2,1:T(8,128)(2,1)}, u32[]{:S(2)}) copy-start(bf16[128,8,576]{0,2,1:T(8,128)(2,1)} %param.9) | copy-start | bytes 3538948
